TPU v7x, 32 devices: a whole 2x2x4 slice. The times are simulated.
32 devices in a mesh: gx: 4 (over z), gy: 4 (over y, core), gz: 2 (over x).
Axes of the slice: x: 2, y: 2, z: 4, core: 2. Of those that a mesh axis runs over, the one named last changes fastest.
Arguments:
- gas_position: float32 [3, 131072], P(None, ('gx', 'gy', 'gz')), may hold values from 0 to 1
- gas_mass: float32 [131072], P(('gx', 'gy', 'gz')), may hold values from 0.3 to 3
- gas_smoothing: float32 [131072], P(('gx', 'gy', 'gz')), may hold values from 0.5 to 1.5
- leaf_counts: int32 [1024], P(('gx', 'gy', 'gz')), may hold values from 64 to 128
- ghost_lists: int32 [32, 4, 2], P(('gx', 'gy', 'gz')), may hold values from 0 to 31, as said below
- star_position: float32 [3, 65536], P(None, ('gx', 'gy', 'gz')), may hold values from 0 to 1
- star_energy: float32 [65536], P(('gx', 'gy', 'gz')), may hold values from 0.1 to 10
- star_momentum: float32 [3, 65536], P(None, ('gx', 'gy', 'gz')), may hold values from -6 to 6
- block_counts: int32 [512], P(('gx', 'gy', 'gz')), may hold values from 1 to 128
- block_owners: int32 [512, 1], P(('gx', 'gy', 'gz')), may hold values from 0 to 7; in each aligned block of 16 rows (0 to 15, 16 to 31, ...) at most 3 rows name the same one
- block_leaves: int32 [512], P(('gx', 'gy', 'gz')), may hold values from 0 to 31
Outputs:
- accel: float32 [3, 131072], P(None, ('gx', 'gy', 'gz'))
- deposit: float32 [4, 131072], P(None, ('gx', 'gy', 'gz'))
Inputs may be any that keep to these rules, and one draw needn't show every extreme that they name: `ghost_lists`: each of the four lists of a device names 2 different leaves. `block_owners`: among the 16 star blocks of one device, no owner is named more than 3 times, and in some devices one owner is named exactly 3 times.
All inputs are finite; a program needn't handle non-finite values.
Results may differ from a plain program's by a relative error of at most 0.00015.
Values sent between devices are 32-bit elements; how exact they have to be, the bound alone decides.
A program may use at most 64 MiB of HBM per device.

v0:
```python
import functools
import math

import jax
import jax.numpy as jnp
from jax import lax
from jax.experimental import pallas as pl
from jax.experimental.pallas import tpu as pltpu
from jax.sharding import PartitionSpec as P

LANES = 128
SLOTS = 3
SPLIT_SQ = 1.0
SOFT_SQ = 0.01
GRAVITY = 0.002
RADIAL_PUSH = 1.0

SCALE = math.log2(math.e) / (1.5 * SPLIT_SQ)
FACTOR = GRAVITY * math.exp(SOFT_SQ / SPLIT_SQ) * SCALE**1.5
FEATURES = 40
MESH = pl.DeviceIdType.MESH
HIGHEST = lax.Precision.HIGHEST
F32 = jnp.float32
BF16 = jnp.bfloat16

TARGETS = 1024
SOURCES = 256
UNROLL = 2


def split3(x):
    a = x.astype(BF16).astype(F32)
    rest = x - a
    b = rest.astype(BF16).astype(F32)
    return a, b, rest - b


def prepare_sends(
    sizes,
    pos_ref, mass_ref, count_ref, ghost_ref,
    star_pos_ref, energy_ref, star_mom_ref, block_count_ref, owner_ref, leaf_ref,
    src, ghost_send, star_send,
):
    n_x, n_y, n_z, leaves, ghosts, blocks = sizes
    owners = n_y * n_z
    rows = leaves * LANES
    lane = lax.broadcasted_iota(jnp.int32, (1, LANES), 1)

    src[0:3, :] = pos_ref[...]
    src[4:8, :] = jnp.zeros((4, rows), F32)
    for l in range(leaves):
        here = slice(l * LANES, (l + 1) * LANES)
        alive = lane < count_ref[l]
        src[3:4, here] = jnp.where(alive, mass_ref[l : l + 1, :], 0.0)
        src[4:5, here] = jnp.where(alive, 1.0, 0.0).astype(F32)
    for k in range(4):
        for g in range(ghosts):
            start = pl.multiple_of(ghost_ref[k * ghosts + g] * LANES, LANES)
            ghost_send[k, :, g * LANES : (g + 1) * LANES] = src[:, pl.ds(start, LANES)]

    @pl.loop(0, owners)
    def _(o):
        def scan(b, found):
            hit = owner_ref[b] == o
            i0, i1, i2 = found
            return (jnp.where(hit, b, i0), jnp.where(hit, i0, i1), jnp.where(hit, i1, i2))

        none = jnp.int32(-1)
        found = lax.fori_loop(0, blocks, scan, (none,) * SLOTS, unroll=8)
        for k in range(SLOTS):
            b = jnp.maximum(found[k], 0)
            valid = found[k] >= 0
            start = pl.multiple_of(b * LANES, LANES)
            live = lane < jnp.where(valid, block_count_ref[b], 0)
            named = lane == jnp.where(valid, leaf_ref[b], -1)
            star_send[o, k, 0:3] = star_pos_ref[:, pl.ds(start, LANES)]
            star_send[o, k, 3:4] = jnp.where(live, energy_ref[pl.ds(b, 1), :], 0.0)
            star_send[o, k, 4:7] = jnp.where(live, star_mom_ref[:, pl.ds(start, LANES)], 0.0)
            star_send[o, k, 7:8] = jnp.where(named, 1.0, 0.0).astype(F32)


def kernel(
    sizes,
    own_ref, smooth_ref, ghost_send, star_send,
    accel_ref, deposit_ref,
    src, ghost_recv, star_recv,
    feat, side_a, side_b, weights, acc, table, marker, gathered, dep,
    ghost_ssem, ghost_rsem, star_ssem, star_rsem,
):
    n_x, n_y, n_z, leaves, ghosts, blocks = sizes
    owners = n_y * n_z
    rows = leaves * LANES
    wide = ghosts * LANES
    x, y, z = lax.axis_index("gx"), lax.axis_index("gy"), lax.axis_index("gz")
    me = y * n_z + z

    def owner_at(d):
        other = lax.rem(me + d, owners)
        return other, (x, lax.div(other, n_z), lax.rem(other, n_z))

    def beside(k):
        step = 1 if k % 2 == 0 else -1
        if k < 2:
            return (lax.rem(x + step + n_x, n_x), y, z)
        return (x, lax.rem(y + step + n_y, n_y), z)

    barrier = pltpu.get_barrier_semaphore()
    for k in range(2):
        pl.semaphore_signal(barrier, inc=1, device_id=beside(k), device_id_type=MESH)

    @pl.loop(1, owners)
    def _(d):
        pl.semaphore_signal(barrier, inc=1, device_id=owner_at(d)[1], device_id_type=MESH)

    src[:, 0:rows] = own_ref[...]
    pl.semaphore_wait(barrier, owners + 1)

    def ghost_copy(k):
        return pltpu.make_async_remote_copy(
            src_ref=ghost_send.at[k], dst_ref=ghost_recv.at[k],
            send_sem=ghost_ssem.at[k], recv_sem=ghost_rsem.at[k],
            device_id=beside(k), device_id_type=MESH,
        )

    def star_copy(d):
        other, where = owner_at(d)
        return pltpu.make_async_remote_copy(
            src_ref=star_send.at[other], dst_ref=star_recv.at[me],
            send_sem=star_ssem.at[d], recv_sem=star_rsem.at[d],
            device_id=where, device_id_type=MESH,
        )

    for k in range(4):
        ghost_copy(k).start()

    @pl.loop(1, owners)
    def _(d):
        star_copy(d).start()

    star_recv[me] = star_send[me]

    def put(rows_of):
        at = 0
        for piece in rows_of:
            feat[at : at + piece.shape[0], :] = piece
            at += piece.shape[0]
        if at < FEATURES:
            feat[at:FEATURES, :] = jnp.zeros((FEATURES - at, SOURCES), F32)

    def prepare(start, targets):
        here = pl.ds(start, SOURCES)
        u = src[0:3, here] - 0.5
        mass = src[3:4, here]
        norm = SCALE * jnp.sum(u * u, axis=0, keepdims=True)
        a = split3((-2.0 * SCALE) * u)
        n = split3(norm + SCALE * SOFT_SQ)
        one = jnp.ones((1, SOURCES), F32)
        put([a[0]] * 3 + [a[1]] * 3 + [a[2]] * 3 + list(n) + [one] * 3)
        side_a[here, :] = feat[...].T.astype(BF16)
        wx, wm = split3(mass * u), split3(mass)
        put([wx[0], wm[0], wx[1], wm[1], wx[2], wm[2]])
        weights[:, here] = feat[0:16, :].astype(BF16)
        if targets:
            b = split3(u)
            put(list(b) * 3 + [one] * 3 + list(split3(norm)))
            side_b[:, here] = feat[...].astype(BF16)

    @pl.loop(0, rows // SOURCES)
    def _(c):
        prepare(pl.multiple_of(c * SOURCES, SOURCES), True)

    def pairs(start, right):
        d = jnp.dot(
            side_a[pl.ds(start, SOURCES), :], right, preferred_element_type=F32
        )
        value = jnp.exp2(-1.5 * (d + lax.log2(d)))
        high = value.astype(BF16)
        low = (value - high.astype(F32)).astype(BF16)
        w = weights[:, pl.ds(start, SOURCES)]
        return jnp.dot(w, high, preferred_element_type=F32) + jnp.dot(
            w, low, preferred_element_type=F32
        )

    def over(first, count, right, total, unroll):
        def step(c, total):
            start = pl.multiple_of(first + c * SOURCES, SOURCES)
            return total + pairs(start, right)

        return lax.fori_loop(0, count, step, total, unroll=unroll)

    @pl.loop(0, rows // TARGETS)
    def _(t):
        here = pl.ds(pl.multiple_of(t * TARGETS, TARGETS), TARGETS)
        acc[:, here] = over(
            0, rows // SOURCES, side_b[:, here], jnp.zeros((16, TARGETS), F32), UNROLL
        )

    for k in range(4):
        ghost_copy(k).wait()
        there = slice(rows + k * wide, rows + (k + 1) * wide)
        src[:, there] = ghost_recv[k]
        shifted = slice(k // 2, k // 2 + 1)
        src[shifted, there] = src[shifted, there] + (-1.0 if k % 2 == 0 else 1.0)

    @pl.loop(0, 4 * wide // SOURCES)
    def _(c):
        prepare(pl.multiple_of(rows + c * SOURCES, SOURCES), False)

    @pl.loop(0, rows // TARGETS)
    def _(t):
        here = pl.ds(pl.multiple_of(t * TARGETS, TARGETS), TARGETS)
        total = over(rows, 4 * wide // SOURCES, side_b[:, here], acc[:, here], True)
        total = total[0:4] + total[4:8] + total[8:12]
        u = src[0:3, here] - 0.5
        value = FACTOR * (total[0:3] - u * total[3:4])
        accel_ref[:, here] = jnp.where(src[4:5, here] > 0.5, value, 0.0)

    h = smooth_ref[...]
    table[:, 3 * LANES :] = 1.0 / (h * h)
    for l in range(leaves):
        for c in range(3):
            table[l : l + 1, c * LANES : (c + 1) * LANES] = src[
                c : c + 1, l * LANES : (l + 1) * LANES
            ]

    @pl.loop(1, owners)
    def _(d):
        star_copy(d).wait()

    @pl.loop(0, owners)
    def _(o):
        for k in range(SLOTS):
            marker[pl.ds(o * SLOTS + k, 1), :] = star_recv[o, k, 7:8]

    for c in range(4):
        gathered[c] = jnp.dot(
            marker[:, 0:leaves],
            table[:, c * LANES : (c + 1) * LANES],
            precision=HIGHEST,
            preferred_element_type=F32,
        )

    @pl.loop(0, owners)
    def _(o):
        for k in range(SLOTS):
            at = pl.ds(o * SLOTS + k, 1)
            star = star_recv[o, k].T
            gas = [gathered[c, at, :] for c in range(4)]
            seps = [gas[c] - star[:, c : c + 1] for c in range(3)]
            distance = seps[0] * seps[0] + seps[1] * seps[1] + seps[2] * seps[2]
            weight = jnp.exp(-distance * gas[3])
            share = weight / (1.0 + jnp.sum(weight, axis=1, keepdims=True))
            heat = star[:, 3:4] * share
            dep[0, at, :] = jnp.sum(heat, axis=0, keepdims=True)
            for c in range(3):
                kick = share * star[:, 4 + c : 5 + c] + RADIAL_PUSH * heat * seps[c]
                dep[c + 1, at, :] = jnp.sum(kick, axis=0, keepdims=True)

    named = marker[...].T[0:leaves]
    for c in range(4):
        table[:, c * LANES : (c + 1) * LANES] = jnp.dot(
            named, dep[c], precision=HIGHEST, preferred_element_type=F32
        )
    for l in range(leaves):
        alive = src[4:5, l * LANES : (l + 1) * LANES] > 0.5
        for c in range(4):
            deposit_ref[c : c + 1, l * LANES : (l + 1) * LANES] = jnp.where(
                alive, table[l : l + 1, c * LANES : (c + 1) * LANES], 0.0
            )


def on_device(
    mesh_sizes,
    gas_position, gas_mass, gas_smoothing, leaf_counts, ghost_lists,
    star_position, star_energy, star_momentum, block_counts, block_owners, block_leaves,
):
    n_x, n_y, n_z = mesh_sizes
    leaves = leaf_counts.shape[0]
    blocks = block_counts.shape[0]
    ghosts = ghost_lists.shape[2]
    rows = leaves * LANES
    owners = n_y * n_z
    slots = owners * SLOTS
    slot_rows = -(-slots // 8) * 8
    total = rows + 4 * ghosts * LANES
    vmem = pl.BlockSpec(memory_space=pltpu.VMEM)
    smem = pl.BlockSpec(memory_space=pltpu.SMEM)
    sizes = (n_x, n_y, n_z, leaves, ghosts, blocks)
    own, ghost_send, star_send = pl.pallas_call(
        functools.partial(prepare_sends, sizes),
        out_shape=(
            jax.ShapeDtypeStruct((8, rows), F32),
            jax.ShapeDtypeStruct((4, 8, ghosts * LANES), F32),
            jax.ShapeDtypeStruct((owners, SLOTS, 8, LANES), F32),
        ),
        in_specs=[vmem, vmem, smem, smem, vmem, vmem, vmem, smem, smem, smem],
        out_specs=(vmem, vmem, vmem),
    )(
        gas_position,
        gas_mass.reshape(leaves, LANES),
        leaf_counts,
        ghost_lists.reshape(-1),
        star_position,
        star_energy.reshape(blocks, LANES),
        star_momentum,
        block_counts,
        block_owners.reshape(-1),
        block_leaves,
    )
    return pl.pallas_call(
        functools.partial(kernel, sizes),
        out_shape=(
            jax.ShapeDtypeStruct((3, rows), F32),
            jax.ShapeDtypeStruct((4, rows), F32),
        ),
        in_specs=[vmem, vmem, vmem, vmem],
        out_specs=(vmem, vmem),
        scratch_shapes=[
            pltpu.VMEM((8, total), F32),
            pltpu.VMEM((4, 8, ghosts * LANES), F32),
            pltpu.VMEM((owners, SLOTS, 8, LANES), F32),
            pltpu.VMEM((FEATURES, SOURCES), F32),
            pltpu.VMEM((total, FEATURES), BF16),
            pltpu.VMEM((FEATURES, rows), BF16),
            pltpu.VMEM((16, total), BF16),
            pltpu.VMEM((16, rows), F32),
            pltpu.VMEM((leaves, 4 * LANES), F32),
            pltpu.VMEM((slot_rows, LANES), F32),
            pltpu.VMEM((4, slot_rows, LANES), F32),
            pltpu.VMEM((4, slot_rows, LANES), F32),
            pltpu.SemaphoreType.DMA((4,)),
            pltpu.SemaphoreType.DMA((4,)),
            pltpu.SemaphoreType.DMA((owners,)),
            pltpu.SemaphoreType.DMA((owners,)),
        ],
        compiler_params=pltpu.CompilerParams(collective_id=0, has_side_effects=True),
    )(own, gas_smoothing.reshape(leaves, LANES), ghost_send, star_send)


def solution(mesh):
    split = ("gx", "gy", "gz")
    placed = (
        P(None, split), P(split), P(split), P(split), P(split, None, None),
        P(None, split), P(split), P(None, split), P(split), P(split, None), P(split),
    )
    sizes = tuple(mesh.shape[axis] for axis in split)
    return jax.shard_map(
        functools.partial(on_device, sizes),
        mesh=mesh,
        in_specs=placed,
        out_specs=(P(None, split), P(None, split)),
        check_vma=False,
    )
```

profile of v0, /device:TPU:0, one launch (start us, length us, event | category | flops | bytes accessed | tf_op | source)
XLA Modules:
  0.0 68.3 jit_solution(17068169215415798605)
XLA Ops:
  0.6 0.0 copy-start.1
  0.6 0.7 copy-done.1
  1.3 0.1 copy.14
  1.4 0.6 reshape.20.ghost_ref
  2.0 2.0 %shard_map.122 = (f32[8,4096]{1,0:T(8,128)}, f32[4,8,256]{2,1,0:T(8,128)}, f32[8,3,8,128]{3,2,1,0:T(8,128)}) custom-call(f32[3,4096]{1,0:T(4,128)} %pos_ref.1, f32[32,128]{1,0:T(8,128)} %bitcast.4, s32[32]{0:T(128)} %count_ref.1, s32[8]{0:T(128)} %reshape.20.ghost_ref, f32[3,2048]{1,0:T(4,128)} %star_pos_ref.1, f32[16,128]{1,0:T(8,128)} %bitcast.6, ...), custom_call_target="tpu_custom_call" | custom-call | tf_op jit(solution)/shard_map/pallas_call | solution.py:289
  4.0 62.1 %shard_map.123 = (f32[3,4096]{1,0:T(4,128)}, f32[4,4096]{1,0:T(4,128)}) custom-call(f32[8,4096]{1,0:T(8,128)} %get-tuple-element.5.own_ref, f32[32,128]{1,0:T(8,128)} %bitcast.5, f32[4,8,256]{2,1,0:T(8,128)} %get-tuple-element.6.ghost_send, f32[8,3,8,128]{3,2,1,0:T(8,128)} %get-tuple-element.7.star_send), custom_call_target="tpu_custom_call" | custom-call | tf_op jit(solution)/shard_map/pallas_call | solution.py:310
  66.2 0.0 copy-start
  66.2 1.5 %copy.17 = f32[3,4096]{1,0:T(4,128)} copy(f32[3,4096]{1,0:T(4,128)} %get-tuple-element.10) | data formatting | bytes 98304
  67.7 0.0 copy-done
  67.7 0.6 copy.18
Async XLA Ops:
  0.6 0.7 copy-start.1
  66.2 1.5 %copy-start = (f32[4,4096]{1,0:T(4,128)S(1)}, f32[4,4096]{1,0:T(4,128)}, u32[]{:S(2)}) copy-start(f32[4,4096]{1,0:T(4,128)} %get-tuple-element.11) | copy-start | bytes 196612
where the time goes:
time: 68.6 us; the launch traced here: 68.3 us
  Pallas kernels  64.2 us (94%)
  local copies, waits for them, and re-layouts  3.51 us (5%)
    pallas_call x1, Pallas kernels, on_device(): pl.pallas_call(functools.partial(kernel, sizes), out_shape=(jax.ShapeDtyp...  62.1 us
    unnamed x7, local copies, waits for them, and re-layouts  2.91 us
    pallas_call x1, Pallas kernels, on_device(): pl.pallas_call(functools.partial(prepare_sends, sizes), out_shape=(jax.Sh...  2.03 us

commit v1 on v0

v1 whole, which is shorter than its diff:
```python
import functools
import math

import jax
import jax.numpy as jnp
import numpy as np
from jax import lax
from jax.experimental import pallas as pl
from jax.experimental.pallas import tpu as pltpu
from jax.sharding import PartitionSpec as P

LANES = 128
SLOTS = 3
SPLIT_SQ = 1.0
SOFT_SQ = 0.01
GRAVITY = 0.002
RADIAL_PUSH = 1.0

LOG2E = math.log2(math.e)
SCALE = LOG2E / (1.5 * SPLIT_SQ)
FACTOR = GRAVITY * math.exp(SOFT_SQ / SPLIT_SQ) * SCALE**1.5
MESH = pl.DeviceIdType.MESH
F32 = jnp.float32
BF16 = jnp.bfloat16

TILE = 256
FEATURES = 48
UNROLL = 8


def split3(x):
    a = x.astype(BF16).astype(F32)
    rest = x - a
    b = rest.astype(BF16).astype(F32)
    return a, b, rest - b


def prepare_sends(
    sizes,
    pos_ref, mass_ref, count_ref, ghost_ref,
    star_pos_ref, energy_ref, star_mom_ref, block_count_ref, owner_ref, leaf_ref,
    own, ghost_send, star_send,
):
    n_x, n_y, n_z, leaves, ghosts, blocks = sizes
    owners = n_y * n_z
    rows = leaves * LANES
    lane = lax.broadcasted_iota(jnp.int32, (1, LANES), 1)

    own[0:3, :] = pos_ref[...]
    own[4:8, :] = jnp.zeros((4, rows), F32)
    for l in range(leaves):
        here = slice(l * LANES, (l + 1) * LANES)
        alive = lane < count_ref[l]
        own[3:4, here] = jnp.where(alive, mass_ref[l : l + 1, :], 0.0)
    for k in range(4):
        for g in range(ghosts):
            leaf = ghost_ref[k * ghosts + g]
            start = pl.multiple_of(leaf * LANES, LANES)
            here = slice(g * LANES, (g + 1) * LANES)
            ghost_send[k, :, here] = own[:, pl.ds(start, LANES)]
            ghost_send[k, 7:8, here] = jnp.full((1, LANES), count_ref[leaf].astype(F32))

    @pl.loop(0, owners)
    def _(o):
        def scan(b, found):
            hit = owner_ref[b] == o
            i0, i1, i2 = found
            return (jnp.where(hit, b, i0), jnp.where(hit, i0, i1), jnp.where(hit, i1, i2))

        none = jnp.int32(-1)
        found = lax.fori_loop(0, blocks, scan, (none,) * SLOTS, unroll=8)
        for k in range(SLOTS):
            b = jnp.maximum(found[k], 0)
            valid = found[k] >= 0
            start = pl.multiple_of(b * LANES, LANES)
            count = jnp.where(valid, block_count_ref[b], 0)
            live = lane < count
            leaf = leaf_ref[b].astype(F32)
            star_send[o, k, 0:3] = star_pos_ref[:, pl.ds(start, LANES)]
            star_send[o, k, 3:4] = jnp.where(live, energy_ref[pl.ds(b, 1), :], 0.0)
            star_send[o, k, 4:7] = jnp.where(live, star_mom_ref[:, pl.ds(start, LANES)], 0.0)
            star_send[o, k, 7:8] = jnp.where(lane == 0, leaf, count.astype(F32))


def exchange(
    sizes,
    ghost_send, star_send,
    ghost_recv, star_recv, meta,
    ghost_ssem, ghost_rsem, star_ssem, star_rsem,
):
    n_x, n_y, n_z, leaves, ghosts, blocks = sizes
    owners = n_y * n_z
    x, y, z = lax.axis_index("gx"), lax.axis_index("gy"), lax.axis_index("gz")
    me = y * n_z + z

    def owner_at(d):
        other = lax.rem(me + d, owners)
        return other, (x, lax.div(other, n_z), lax.rem(other, n_z))

    def beside(k):
        step = 1 if k % 2 == 0 else -1
        if k < 2:
            return (lax.rem(x + step + n_x, n_x), y, z)
        return (x, lax.rem(y + step + n_y, n_y), z)

    barrier = pltpu.get_barrier_semaphore()
    for k in range(2):
        pl.semaphore_signal(barrier, inc=1, device_id=beside(k), device_id_type=MESH)

    @pl.loop(1, owners)
    def _(d):
        pl.semaphore_signal(barrier, inc=1, device_id=owner_at(d)[1], device_id_type=MESH)

    pl.semaphore_wait(barrier, owners + 1)

    def ghost_copy(k):
        return pltpu.make_async_remote_copy(
            src_ref=ghost_send.at[k], dst_ref=ghost_recv.at[k],
            send_sem=ghost_ssem.at[k], recv_sem=ghost_rsem.at[k],
            device_id=beside(k), device_id_type=MESH,
        )

    def star_copy(d):
        other, where = owner_at(d)
        return pltpu.make_async_remote_copy(
            src_ref=star_send.at[other], dst_ref=star_recv.at[me],
            send_sem=star_ssem.at[d], recv_sem=star_rsem.at[d],
            device_id=where, device_id_type=MESH,
        )

    @pl.loop(1, owners)
    def _(d):
        star_copy(d).start()

    for k in range(4):
        ghost_copy(k).start()
    star_recv[me] = star_send[me]
    for k in range(4):
        ghost_copy(k).wait()

    @pl.loop(1, owners)
    def _(d):
        star_copy(d).wait()

    for k in range(4):
        for g in range(ghosts):
            at = k * ghosts + g
            meta[at : at + 1, :] = ghost_recv[k, 7:8, g * LANES : (g + 1) * LANES]

    @pl.loop(0, owners)
    def _(o):
        for k in range(SLOTS):
            meta[pl.ds(4 * ghosts + o * SLOTS + k, 1), :] = star_recv[o, k, 7:8]


def gravity(
    sizes,
    count_ref, meta_ref, first_ref, second_ref,
    own_ref, smooth_ref, ghost_ref, star_ref,
    accel_ref, deposit_ref,
    comp, side_a, side_b, weights, acc, res,
    d0, d1, h0, h1, l0, l1,
    offsets, one_i, one_j, slots,
):
    n_x, n_y, n_z, leaves, ghosts, blocks = sizes
    owners = n_y * n_z
    rows = leaves * LANES
    capacity = comp.shape[1]
    trash = acc.shape[1] // TILE - 1
    lane = lax.broadcasted_iota(jnp.int32, (8, LANES), 1)
    sub = lax.broadcasted_iota(jnp.int32, (8, LANES), 0)
    wide_sub = lax.broadcasted_iota(jnp.int32, (8, TILE), 0)

    def place(tile, count, off, current):
        turn = lax.rem(off, LANES)
        base = pl.multiple_of(off - turn, LANES)
        rolled = pltpu.roll(tile, turn, 1)
        current = jnp.where(lane >= turn, rolled, current)
        comp[:, pl.ds(base, LANES)] = current
        return off + count, jnp.where(turn + count >= LANES, rolled, current)

    def own_leaf(l, carry):
        offsets[l] = carry[0]
        start = pl.multiple_of(l * LANES, LANES)
        return place(own_ref[:, pl.ds(start, LANES)], count_ref[l], *carry)

    carry = lax.fori_loop(
        0, leaves, own_leaf, (jnp.int32(0), jnp.zeros((8, LANES), F32)), unroll=8
    )
    n_own = carry[0]
    for k in range(4):
        shift = jnp.where(sub == k // 2, -1.0 if k % 2 == 0 else 1.0, 0.0)
        for g in range(ghosts):
            tile = ghost_ref[k, :, g * LANES : (g + 1) * LANES] + shift
            count = meta_ref[k * ghosts + g, 0].astype(jnp.int32)
            carry = place(tile, count, *carry)
    n_all, current = carry
    turn = lax.rem(n_all, LANES)
    base = n_all - turn
    comp[:, pl.ds(pl.multiple_of(base, LANES), LANES)] = jnp.where(lane < turn, current, 0.0)
    for extra in range(1, TILE // LANES):
        at = pl.multiple_of(base + extra * LANES, LANES)
        comp[:, pl.ds(at, LANES)] = jnp.zeros((8, LANES), F32)
    targets = lax.div(n_own + (TILE - 1), TILE)
    sources = lax.div(n_all + (TILE - 1), TILE)

    def features(parts):
        return jnp.concatenate(parts, axis=0)

    def prepare(c, _):
        here = pl.ds(pl.multiple_of(c * TILE, TILE), TILE)
        tile = comp[:, here]
        u = tile - 0.5
        mass = tile[3:4]
        norm = SCALE * (u[0:1] * u[0:1] + u[1:2] * u[1:2] + u[2:3] * u[2:3])
        one = jnp.where(wide_sub == 4, 1.0, 0.0)
        left = jnp.where(
            wide_sub < 3, (-2.0 * SCALE) * u, jnp.where(wide_sub == 3, norm + SCALE * SOFT_SQ, one)
        )
        p0, p1, p2 = split3(left)
        side_a[here, :] = features([p0, p0, p1, p1, p0, p2]).T.astype(BF16)
        one = jnp.where(wide_sub == 3, 1.0, 0.0)
        right = jnp.where(wide_sub < 3, u, jnp.where(wide_sub == 4, norm, one))
        q0, q1, q2 = split3(right)
        side_b[:, here] = features([q0, q1, q0, q1, q2, q0]).astype(BF16)
        w0, w1, w2 = split3(jnp.where(wide_sub < 3, mass * u, jnp.where(wide_sub == 3, mass, 0.0)))
        w02 = jnp.where(wide_sub < 4, w0, pltpu.roll(w2, 4, 0))
        weights[:, here] = features([w02, w1]).astype(BF16)
        acc[:, here] = jnp.zeros((16, TILE), F32)
        return 0

    lax.fori_loop(0, sources, prepare, 0)

    distance, high, low = (d0, d1), (h0, h1), (l0, l1)

    def at(block):
        return pl.ds(pl.multiple_of(block * TILE, TILE), TILE)

    def nn(a, b):
        return jnp.dot(a, b, preferred_element_type=F32)

    def nt(a, b):
        return lax.dot_general(a, b, (((1,), (1,)), ((), ())), preferred_element_type=F32)

    def tiles(table_i, table_j, count, both):
        def step(p, even):
            q = jnp.maximum(p - 2, 0)
            valid = jnp.logical_and(p >= 2, p - 2 < count)
            i, j = table_i[q], table_j[q]
            to_i = at(jnp.where(valid, i, trash))
            h, l = high[even][...], low[even][...]
            w = weights[:, at(j)]
            acc[:, to_i] = acc[:, to_i] + (nn(w, h) + nn(w, l))
            if both:
                to_j = at(jnp.where(valid, j, trash))
                w = weights[:, at(i)]
                acc[:, to_j] = acc[:, to_j] + (nt(w, h) + nt(w, l))
            d = distance[1 - even][...]
            value = jnp.exp2(-1.5 * (d + lax.log2(d)))
            h = value.astype(BF16)
            high[1 - even][...] = h
            low[1 - even][...] = (value - h.astype(F32)).astype(BF16)
            distance[even][...] = nn(side_a[at(table_j[p]), :], side_b[:, at(table_i[p])])

        @pl.loop(0, lax.div(count + 2 + UNROLL - 1, UNROLL))
        def _(g):
            for u in range(UNROLL):
                step(g * UNROLL + u, u % 2)

    def diagonal(i, n):
        one_i[n] = i
        one_j[n] = i
        return n + 1

    def column(s, n):
        def entry(i, n):
            one_i[n] = i
            one_j[n] = s
            return n + 1

        return lax.fori_loop(0, targets, entry, n)

    single = lax.fori_loop(0, targets, diagonal, jnp.int32(0))
    single = lax.fori_loop(targets, sources, column, single)
    for e in range(UNROLL + 2):
        one_i[single + e] = 0
        one_j[single + e] = 0

    tiles(first_ref, second_ref, lax.div(targets * (targets - 1), 2), True)
    tiles(one_i, one_j, single, False)

    def finish(c, _):
        here = pl.ds(pl.multiple_of(c * TILE, TILE), TILE)
        head, tail = acc[0:8, here], acc[8:16, here]
        total = head + pltpu.roll(head, 4, 0) + tail
        res[:, here] = FACTOR * (total - (comp[:, here] - 0.5) * total[3:4])
        return 0

    lax.fori_loop(0, targets, finish, 0)

    def spread(l, _):
        off = offsets[l]
        turn = lax.rem(off, LANES)
        base = pl.multiple_of(off - turn, LANES)
        both = jnp.where(
            lane >= turn,
            res[:, pl.ds(base, LANES)],
            res[:, pl.ds(pl.multiple_of(base + LANES, LANES), LANES)],
        )
        back = pltpu.roll(both, lax.rem(LANES - turn, LANES), 1)
        start = pl.multiple_of(l * LANES, LANES)
        accel_ref[:, pl.ds(start, LANES)] = jnp.where(lane < count_ref[l], back, 0.0)[0:3]
        deposit_ref[:, pl.ds(start, LANES)] = jnp.zeros((4, LANES), F32)
        return 0

    lax.fori_loop(0, leaves, spread, 0, unroll=8)

    def valid_slot(s, n):
        slots[n] = s
        return n + jnp.where(meta_ref[4 * ghosts + s, 1] > 0.5, 1, 0)

    n_slots = lax.fori_loop(0, owners * SLOTS, valid_slot, jnp.int32(0))
    group = 4
    for e in range(group):
        slots[n_slots + e] = 0

    def heat(n):
        s = slots[n]
        star = star_ref[s]
        leaf = meta_ref[4 * ghosts + s, 0].astype(jnp.int32)
        there = pl.ds(pl.multiple_of(leaf * LANES, LANES), LANES)
        gas = own_ref[:, there] - 0.5
        h = smooth_ref[pl.ds(leaf, 1), :]
        inverse = LOG2E / (h * h)
        ys = star - 0.5
        gas_norm = gas[0:1] * gas[0:1] + gas[1:2] * gas[1:2] + gas[2:3] * gas[2:3]
        star_norm = ys[0:1] * ys[0:1] + ys[1:2] * ys[1:2] + ys[2:3] * ys[2:3]
        left = jnp.where(
            sub < 3,
            (2.0 * inverse) * gas,
            jnp.where(sub == 3, -inverse * gas_norm, jnp.where(sub == 4, -inverse, 0.0)),
        )
        right = jnp.where(
            sub < 3, ys, jnp.where(sub == 3, 1.0, jnp.where(sub == 4, star_norm, 0.0))
        )
        p0, p1, p2 = split3(left)
        q0, q1, q2 = split3(right)
        a = features([p0, p0, p1, p1, p0, p2]).T.astype(BF16)
        b = features([q0, q1, q0, q1, q2, q0]).astype(BF16)
        weight = jnp.exp2(nn(a, b))
        share = 1.0 / (1.0 + jnp.sum(weight, axis=0, keepdims=True))
        energy = star[3:4]
        momentum = pltpu.roll(star, 4, 0)
        value = jnp.where(sub < 3, momentum - RADIAL_PUSH * energy * ys, energy) * share
        value = jnp.where(sub < 4, value, 0.0)
        v0, v1, v2 = split3(value)
        v02 = jnp.where(sub < 4, v0, pltpu.roll(v2, 4, 0))
        v = features([v02, v1]).astype(BF16)
        hi = weight.astype(BF16)
        lo = (weight - hi.astype(F32)).astype(BF16)
        out = nt(v, hi) + nt(v, lo)
        head, tail = out[0:8], out[8:16]
        total = head + pltpu.roll(head, 4, 0) + tail
        heat_here = total[3:4]
        kick = pltpu.roll(total + RADIAL_PUSH * heat_here * gas, 1, 0)
        both = jnp.where(sub == 0, heat_here, kick)
        live = jnp.where(n < n_slots, count_ref[leaf], 0)
        return there, jnp.where(lane < live, both, 0.0)[0:4]

    @pl.loop(0, lax.div(n_slots + group - 1, group))
    def _(t):
        done = [heat(t * group + e) for e in range(group)]
        for there, add in done:
            deposit_ref[:, there] = deposit_ref[:, there] + add


def on_device(
    mesh_sizes,
    gas_position, gas_mass, gas_smoothing, leaf_counts, ghost_lists,
    star_position, star_energy, star_momentum, block_counts, block_owners, block_leaves,
):
    n_x, n_y, n_z = mesh_sizes
    leaves = leaf_counts.shape[0]
    blocks = block_counts.shape[0]
    ghosts = ghost_lists.shape[2]
    rows = leaves * LANES
    owners = n_y * n_z
    slots = owners * SLOTS
    wide = ghosts * LANES
    vmem = pl.BlockSpec(memory_space=pltpu.VMEM)
    smem = pl.BlockSpec(memory_space=pltpu.SMEM)
    sizes = (n_x, n_y, n_z, leaves, ghosts, blocks)
    ghost_shape = jax.ShapeDtypeStruct((4, 8, wide), F32)
    star_shape = jax.ShapeDtypeStruct((owners, SLOTS, 8, LANES), F32)
    own, ghost_send, star_send = pl.pallas_call(
        functools.partial(prepare_sends, sizes),
        out_shape=(jax.ShapeDtypeStruct((8, rows), F32), ghost_shape, star_shape),
        in_specs=[vmem, vmem, smem, smem, vmem, vmem, vmem, smem, smem, smem],
        out_specs=(vmem, vmem, vmem),
    )(
        gas_position,
        gas_mass.reshape(leaves, LANES),
        leaf_counts,
        ghost_lists.reshape(-1),
        star_position,
        star_energy.reshape(blocks, LANES),
        star_momentum,
        block_counts,
        block_owners.reshape(-1),
        block_leaves,
    )
    ghost, star, meta = pl.pallas_call(
        functools.partial(exchange, sizes),
        out_shape=(
            ghost_shape,
            star_shape,
            jax.ShapeDtypeStruct((4 * ghosts + slots, LANES), F32),
        ),
        in_specs=[vmem, vmem],
        out_specs=(vmem, vmem, vmem),
        scratch_shapes=[
            pltpu.SemaphoreType.DMA((4,)),
            pltpu.SemaphoreType.DMA((4,)),
            pltpu.SemaphoreType.DMA((owners,)),
            pltpu.SemaphoreType.DMA((owners,)),
        ],
        compiler_params=pltpu.CompilerParams(collective_id=0, has_side_effects=True),
    )(ghost_send, star_send)
    top = -(-rows // TILE)
    capacity = -(-(rows + 4 * wide) // TILE) * TILE + TILE
    spare = UNROLL + 4
    pairs = [(i, j) for j in range(top + 1) for i in range(j)]
    pairs = pairs + [(0, 0)] * spare
    first = jnp.asarray(np.array([a for a, _ in pairs], np.int32))
    second = jnp.asarray(np.array([b for _, b in pairs], np.int32))
    singles = (capacity // TILE) * top + spare
    return pl.pallas_call(
        functools.partial(gravity, sizes),
        out_shape=(
            jax.ShapeDtypeStruct((3, rows), F32),
            jax.ShapeDtypeStruct((4, rows), F32),
        ),
        in_specs=[smem, smem, smem, smem, vmem, vmem, vmem, vmem],
        out_specs=(vmem, vmem),
        scratch_shapes=[
            pltpu.VMEM((8, capacity), F32),
            pltpu.VMEM((capacity, FEATURES), BF16),
            pltpu.VMEM((FEATURES, capacity), BF16),
            pltpu.VMEM((16, capacity), BF16),
            pltpu.VMEM((16, capacity + TILE), F32),
            pltpu.VMEM((8, rows + 2 * TILE), F32),
            pltpu.VMEM((TILE, TILE), F32),
            pltpu.VMEM((TILE, TILE), F32),
            pltpu.VMEM((TILE, TILE), BF16),
            pltpu.VMEM((TILE, TILE), BF16),
            pltpu.VMEM((TILE, TILE), BF16),
            pltpu.VMEM((TILE, TILE), BF16),
            pltpu.SMEM((leaves,), jnp.int32),
            pltpu.SMEM((singles,), jnp.int32),
            pltpu.SMEM((singles,), jnp.int32),
            pltpu.SMEM((slots + 4,), jnp.int32),
        ],
    )(
        leaf_counts, meta, first, second,
        own, gas_smoothing.reshape(leaves, LANES), ghost, star.reshape(slots, 8, LANES),
    )


def solution(mesh):
    split = ("gx", "gy", "gz")
    placed = (
        P(None, split), P(split), P(split), P(split), P(split, None, None),
        P(None, split), P(split), P(None, split), P(split), P(split, None), P(split),
    )
    sizes = tuple(mesh.shape[axis] for axis in split)
    return jax.shard_map(
        functools.partial(on_device, sizes),
        mesh=mesh,
        in_specs=placed,
        out_specs=(P(None, split), P(None, split)),
        check_vma=False,
    )
```

time: 68.6 us -> 42.7 us (0.62)
  Pallas kernels: 64.2 us -> 40.5 us
  local copies, waits for them, and re-layouts: 3.51 us -> 1.36 us
    pallas_call x1 -> x2, Pallas kernels: 62.1 us -> 38.4 us  [the longest x1 27.2 us: on_device(): pl.pallas_call(functools.partial(gravity, sizes), out_shape=(jax.ShapeDty...]
    unnamed x7 -> x3, local copies, waits for them, and re-layouts: 2.91 us -> 0.76 us
where the time goes in v1:
time: 42.7 us; the launch traced here: 42.5 us
  Pallas kernels  40.5 us (95%)
  local copies, waits for them, and re-layouts  1.36 us (3%)
  between operations  0.65 us (2%)
    pallas_call x1, Pallas kernels, on_device(): pl.pallas_call(functools.partial(gravity, sizes), out_shape=(jax.ShapeDty...  27.2 us
    pallas_call x1, Pallas kernels, on_device(): pl.pallas_call(functools.partial(exchange, sizes), out_shape=(ghost_shape...  11.2 us
    pallas_call x1, Pallas kernels, on_device(): pl.pallas_call(functools.partial(prepare_sends, sizes), out_shape=(jax.Sh...  2.04 us

profile of v1, /device:TPU:0, one launch (start us, length us, event | category | flops | bytes accessed | tf_op | source)
XLA Modules:
  0.0 42.5 jit_solution(8234810374454191399)
XLA Ops:
  0.6 0.0 copy-start
  0.6 0.7 %copy-done = s32[1,4,2]{1,2,0:T(2,128)S(1)} copy-done((s32[1,4,2]{1,2,0:T(2,128)S(1)}, s32[1,4,2]{1,2,0:T(2,128)}, u32[]{:S(2)}) %copy-start) | copy-done | bytes 56
  1.3 0.1 copy.16
  1.4 0.6 %reshape.23.ghost_ref = s32[8]{0:T(128)} reshape(s32[1,4,2]{2,1,0:T(4,128)S(1)} %copy.16) | data formatting | bytes 64 | tf_op jit(solution)/shard_map/reshape | solution.py:404
  2.0 2.0 %shard_map.140 = (f32[8,4096]{1,0:T(8,128)}, f32[4,8,256]{2,1,0:T(8,128)}, f32[8,3,8,128]{3,2,1,0:T(8,128)}) custom-call(f32[3,4096]{1,0:T(4,128)} %pos_ref.1, f32[32,128]{1,0:T(8,128)} %bitcast.6, s32[32]{0:T(128)} %count_ref.3, s32[8]{0:T(128)} %reshape.23.ghost_ref, f32[3,2048]{1,0:T(4,128)} %star_pos_ref.1, f32[16,128]{1,0:T(8,128)} %bitcast.8, ...), custom_call_target="tpu_custom_call" | custom-call | tf_op jit(solution)/shard_map/pallas_call | solution.py:395
  4.0 11.2 %shard_map.141 = (f32[4,8,256]{2,1,0:T(8,128)}, f32[8,3,8,128]{3,2,1,0:T(8,128)}, f32[32,128]{1,0:T(8,128)}) custom-call(f32[4,8,256]{2,1,0:T(8,128)} %get-tuple-element.8.ghost_send, f32[8,3,8,128]{3,2,1,0:T(8,128)} %get-tuple-element.9.star_send), custom_call_target="tpu_custom_call" | custom-call | tf_op jit(solution)/shard_map/pallas_call | solution.py:412
  15.2 27.2 %shard_map.142 = (f32[3,4096]{1,0:T(4,128)}, f32[4,4096]{1,0:T(4,128)}) custom-call(s32[32]{0:T(128)} %count_ref.3, f32[32,128]{1,0:T(8,128)} %get-tuple-element.10.meta_ref, s32[148]{0:T(256)} %constant.4.clone.first_ref, s32[148]{0:T(256)} %constant.5.clone.second_ref, f32[8,4096]{1,0:T(8,128)} %get-tuple-element.11.own_ref, f32[32,128]{1,0:T(8,128)} %bitcast.7, ...), custom_call_target="tpu_custom_call" | custom-call | tf_op jit(solution)/shard_map/pallas_call | solution.py:437
Async XLA Ops:
  0.6 0.7 %copy-start = (s32[1,4,2]{1,2,0:T(2,128)S(1)}, s32[1,4,2]{1,2,0:T(2,128)}, u32[]{:S(2)}) copy-start(s32[1,4,2]{1,2,0:T(2,128)} %param.17) | copy-start | bytes 100

commit v2 on v1

--- a/solution.py
+++ b/solution.py
@@ -10,6 +10,7 @@
 from jax.sharding import PartitionSpec as P
 
 LANES = 128
+HALF = 64
 SLOTS = 3
 SPLIT_SQ = 1.0
 SOFT_SQ = 0.01
@@ -33,6 +34,66 @@
     rest = x - a
     b = rest.astype(BF16).astype(F32)
     return a, b, rest - b
+
+
+def nn(a, b):
+    return jnp.dot(a, b, preferred_element_type=F32)
+
+
+def nt(a, b):
+    return lax.dot_general(a, b, (((1,), (1,)), ((), ())), preferred_element_type=F32)
+
+
+def stack(parts):
+    return jnp.concatenate(parts, axis=0)
+
+
+def block_at(block):
+    return pl.ds(pl.multiple_of(block * TILE, TILE), TILE)
+
+
+def prepare_block(c, comp, side_a, side_b, weights, acc):
+    here = block_at(c)
+    sub = lax.broadcasted_iota(jnp.int32, (8, TILE), 0)
+    tile = comp[:, here]
+    u = tile - 0.5
+    mass = tile[3:4]
+    norm = SCALE * (u[0:1] * u[0:1] + u[1:2] * u[1:2] + u[2:3] * u[2:3])
+    one = jnp.where(sub == 4, 1.0, 0.0)
+    left = jnp.where(
+        sub < 3, (-2.0 * SCALE) * u, jnp.where(sub == 3, norm + SCALE * SOFT_SQ, one)
+    )
+    p0, p1, p2 = split3(left)
+    side_a[here, :] = stack([p0, p0, p1, p1, p0, p2]).T.astype(BF16)
+    one = jnp.where(sub == 3, 1.0, 0.0)
+    right = jnp.where(sub < 3, u, jnp.where(sub == 4, norm, one))
+    q0, q1, q2 = split3(right)
+    side_b[:, here] = stack([q0, q1, q0, q1, q2, q0]).astype(BF16)
+    w0, w1, w2 = split3(jnp.where(sub < 3, mass * u, jnp.where(sub == 3, mass, 0.0)))
+    w02 = jnp.where(sub < 4, w0, pltpu.roll(w2, 4, 0))
+    weights[:, here] = stack([w02, w1]).astype(BF16)
+    acc[:, here] = jnp.zeros((16, TILE), F32)
+
+
+def distances(i, j, out, side_a, side_b):
+    out[...] = nn(side_a[block_at(j), :], side_b[:, block_at(i)])
+
+
+def kernel_values(d_ref, high, low):
+    d = d_ref[...]
+    value = jnp.exp2(-1.5 * (d + lax.log2(d)))
+    h = value.astype(BF16)
+    high[...] = h
+    low[...] = (value - h.astype(F32)).astype(BF16)
+
+
+def accumulate(i, j, to_i, to_j, high, low, weights, acc, both):
+    h, l = high[...], low[...]
+    w = weights[:, block_at(j)]
+    acc[:, block_at(to_i)] = acc[:, block_at(to_i)] + (nn(w, h) + nn(w, l))
+    if both:
+        w = weights[:, block_at(i)]
+        acc[:, block_at(to_j)] = acc[:, block_at(to_j)] + (nt(w, h) + nt(w, l))
 
 
 def prepare_sends(
@@ -54,7 +115,7 @@
         own[3:4, here] = jnp.where(alive, mass_ref[l : l + 1, :], 0.0)
     for k in range(4):
         for g in range(ghosts):
-            leaf = ghost_ref[k * ghosts + g]
+            leaf = ghost_ref[g, k]
             start = pl.multiple_of(leaf * LANES, LANES)
             here = slice(g * LANES, (g + 1) * LANES)
             ghost_send[k, :, here] = own[:, pl.ds(start, LANES)]
@@ -84,8 +145,9 @@
 
 def exchange(
     sizes,
-    ghost_send, star_send,
-    ghost_recv, star_recv, meta,
+    own, ghost_send, star_send,
+    ghost_recv, star_recv, meta, comp, side_a, side_b, weights, acc,
+    d0, d1, h0, h1, l0, l1,
     ghost_ssem, ghost_rsem, star_ssem, star_rsem,
 ):
     n_x, n_y, n_z, leaves, ghosts, blocks = sizes
@@ -110,6 +172,14 @@
     @pl.loop(1, owners)
     def _(d):
         pl.semaphore_signal(barrier, inc=1, device_id=owner_at(d)[1], device_id_type=MESH)
+
+    lane = lax.broadcasted_iota(jnp.int32, (8, LANES), 1)
+    for t in range(leaves // 2):
+        left = own[:, 2 * t * LANES : (2 * t + 1) * LANES]
+        right = own[:, (2 * t + 1) * LANES : (2 * t + 2) * LANES]
+        comp[:, t * LANES : (t + 1) * LANES] = jnp.where(
+            lane < HALF, left, pltpu.roll(right, HALF, 1)
+        )
 
     pl.semaphore_wait(barrier, owners + 1)
 
@@ -135,6 +205,36 @@
     for k in range(4):
         ghost_copy(k).start()
     star_recv[me] = star_send[me]
+
+    firm = comp.shape[1] // TILE
+
+    @pl.loop(0, firm)
+    def _(c):
+        prepare_block(c, comp, side_a, side_b, weights, acc)
+
+    distance, high, low = (d0, d1), (h0, h1), (l0, l1)
+
+    def pair(p):
+        i = p % firm
+        return i, (i + 1 + p // firm) % firm
+
+    count = firm * (firm - 1) // 2
+    distances(*pair(0), d0, side_a, side_b)
+    kernel_values(d0, h0, l0)
+    distances(*pair(1), d1, side_a, side_b)
+    unroll = next(u for u in (14, 10, 8, 6, 4, 2, 1) if count % u == 0)
+    assert unroll % 2 == 0
+
+    @pl.loop(0, count // unroll)
+    def _(g):
+        for e in range(unroll):
+            p = g * unroll + e
+            i, j = pair(p)
+            even = e % 2
+            accumulate(i, j, i, j, high[even], low[even], weights, acc, True)
+            kernel_values(distance[1 - even], high[1 - even], low[1 - even])
+            distances(*pair(p + 2), distance[even], side_a, side_b)
+
     for k in range(4):
         ghost_copy(k).wait()
 
@@ -145,22 +245,23 @@
     for k in range(4):
         for g in range(ghosts):
             at = k * ghosts + g
-            meta[at : at + 1, :] = ghost_recv[k, 7:8, g * LANES : (g + 1) * LANES]
+            meta[at : at + 1, :] = ghost_recv[k, 7:8, g * LANES : (g + 1) * LANES].astype(jnp.int32)
 
     @pl.loop(0, owners)
     def _(o):
         for k in range(SLOTS):
-            meta[pl.ds(4 * ghosts + o * SLOTS + k, 1), :] = star_recv[o, k, 7:8]
+            meta[pl.ds(4 * ghosts + o * SLOTS + k, 1), :] = star_recv[o, k, 7:8].astype(jnp.int32)
 
 
 def gravity(
     sizes,
     count_ref, meta_ref, first_ref, second_ref,
     own_ref, smooth_ref, ghost_ref, star_ref,
+    comp_in, a_in, b_in, weights_in, acc_in,
     accel_ref, deposit_ref,
     comp, side_a, side_b, weights, acc, res,
     d0, d1, h0, h1, l0, l1,
-    offsets, one_i, one_j, slots,
+    offsets, one_i, one_j, slots, sems,
 ):
     n_x, n_y, n_z, leaves, ghosts, blocks = sizes
     owners = n_y * n_z
@@ -169,12 +270,23 @@
     trash = acc.shape[1] // TILE - 1
     lane = lax.broadcasted_iota(jnp.int32, (8, LANES), 1)
     sub = lax.broadcasted_iota(jnp.int32, (8, LANES), 0)
-    wide_sub = lax.broadcasted_iota(jnp.int32, (8, TILE), 0)
-
-    def place(tile, count, off, current):
+    settled = comp_in.shape[1]
+    firm = settled // TILE
+
+    copies = [
+        pltpu.make_async_copy(comp_in, comp.at[:, 0:settled], sems.at[0]),
+        pltpu.make_async_copy(a_in, side_a.at[0:settled, :], sems.at[1]),
+        pltpu.make_async_copy(b_in, side_b.at[:, 0:settled], sems.at[2]),
+        pltpu.make_async_copy(weights_in, weights.at[:, 0:settled], sems.at[3]),
+        pltpu.make_async_copy(acc_in, acc.at[:, 0:settled], sems.at[4]),
+    ]
+    for copy in copies:
+        copy.start()
+
+    def place(tile, count, skip, off, current):
         turn = lax.rem(off, LANES)
         base = pl.multiple_of(off - turn, LANES)
-        rolled = pltpu.roll(tile, turn, 1)
+        rolled = pltpu.roll(tile, lax.rem(turn + (LANES - skip), LANES), 1)
         current = jnp.where(lane >= turn, rolled, current)
         comp[:, pl.ds(base, LANES)] = current
         return off + count, jnp.where(turn + count >= LANES, rolled, current)
@@ -182,18 +294,18 @@
     def own_leaf(l, carry):
         offsets[l] = carry[0]
         start = pl.multiple_of(l * LANES, LANES)
-        return place(own_ref[:, pl.ds(start, LANES)], count_ref[l], *carry)
+        return place(own_ref[:, pl.ds(start, LANES)], count_ref[l] - HALF, HALF, *carry)
 
     carry = lax.fori_loop(
-        0, leaves, own_leaf, (jnp.int32(0), jnp.zeros((8, LANES), F32)), unroll=8
+        0, leaves, own_leaf, (jnp.int32(settled), jnp.zeros((8, LANES), F32)), unroll=8
     )
     n_own = carry[0]
     for k in range(4):
         shift = jnp.where(sub == k // 2, -1.0 if k % 2 == 0 else 1.0, 0.0)
         for g in range(ghosts):
             tile = ghost_ref[k, :, g * LANES : (g + 1) * LANES] + shift
-            count = meta_ref[k * ghosts + g, 0].astype(jnp.int32)
-            carry = place(tile, count, *carry)
+            count = meta_ref[k * ghosts + g, 0]
+            carry = place(tile, count, 0, *carry)
     n_all, current = carry
     turn = lax.rem(n_all, LANES)
     base = n_all - turn
@@ -204,68 +316,31 @@
     targets = lax.div(n_own + (TILE - 1), TILE)
     sources = lax.div(n_all + (TILE - 1), TILE)
 
-    def features(parts):
-        return jnp.concatenate(parts, axis=0)
+    for copy in copies:
+        copy.wait()
 
     def prepare(c, _):
-        here = pl.ds(pl.multiple_of(c * TILE, TILE), TILE)
-        tile = comp[:, here]
-        u = tile - 0.5
-        mass = tile[3:4]
-        norm = SCALE * (u[0:1] * u[0:1] + u[1:2] * u[1:2] + u[2:3] * u[2:3])
-        one = jnp.where(wide_sub == 4, 1.0, 0.0)
-        left = jnp.where(
-            wide_sub < 3, (-2.0 * SCALE) * u, jnp.where(wide_sub == 3, norm + SCALE * SOFT_SQ, one)
-        )
-        p0, p1, p2 = split3(left)
-        side_a[here, :] = features([p0, p0, p1, p1, p0, p2]).T.astype(BF16)
-        one = jnp.where(wide_sub == 3, 1.0, 0.0)
-        right = jnp.where(wide_sub < 3, u, jnp.where(wide_sub == 4, norm, one))
-        q0, q1, q2 = split3(right)
-        side_b[:, here] = features([q0, q1, q0, q1, q2, q0]).astype(BF16)
-        w0, w1, w2 = split3(jnp.where(wide_sub < 3, mass * u, jnp.where(wide_sub == 3, mass, 0.0)))
-        w02 = jnp.where(wide_sub < 4, w0, pltpu.roll(w2, 4, 0))
-        weights[:, here] = features([w02, w1]).astype(BF16)
-        acc[:, here] = jnp.zeros((16, TILE), F32)
+        prepare_block(c, comp, side_a, side_b, weights, acc)
         return 0
 
-    lax.fori_loop(0, sources, prepare, 0)
+    lax.fori_loop(firm, sources, prepare, 0)
 
     distance, high, low = (d0, d1), (h0, h1), (l0, l1)
 
-    def at(block):
-        return pl.ds(pl.multiple_of(block * TILE, TILE), TILE)
-
-    def nn(a, b):
-        return jnp.dot(a, b, preferred_element_type=F32)
-
-    def nt(a, b):
-        return lax.dot_general(a, b, (((1,), (1,)), ((), ())), preferred_element_type=F32)
-
-    def tiles(table_i, table_j, count, both):
+    def tiles(table_i, table_j, begin, count, both):
         def step(p, even):
-            q = jnp.maximum(p - 2, 0)
-            valid = jnp.logical_and(p >= 2, p - 2 < count)
+            q = jnp.maximum(p - 2, begin)
+            valid = jnp.logical_and(p >= begin + 2, p - 2 < count)
             i, j = table_i[q], table_j[q]
-            to_i = at(jnp.where(valid, i, trash))
-            h, l = high[even][...], low[even][...]
-            w = weights[:, at(j)]
-            acc[:, to_i] = acc[:, to_i] + (nn(w, h) + nn(w, l))
-            if both:
-                to_j = at(jnp.where(valid, j, trash))
-                w = weights[:, at(i)]
-                acc[:, to_j] = acc[:, to_j] + (nt(w, h) + nt(w, l))
-            d = distance[1 - even][...]
-            value = jnp.exp2(-1.5 * (d + lax.log2(d)))
-            h = value.astype(BF16)
-            high[1 - even][...] = h
-            low[1 - even][...] = (value - h.astype(F32)).astype(BF16)
-            distance[even][...] = nn(side_a[at(table_j[p]), :], side_b[:, at(table_i[p])])
-
-        @pl.loop(0, lax.div(count + 2 + UNROLL - 1, UNROLL))
+            to_i, to_j = jnp.where(valid, i, trash), jnp.where(valid, j, trash)
+            accumulate(i, j, to_i, to_j, high[even], low[even], weights, acc, both)
+            kernel_values(distance[1 - even], high[1 - even], low[1 - even])
+            distances(table_i[p], table_j[p], distance[even], side_a, side_b)
+
+        @pl.loop(0, lax.div(count - begin + 2 + UNROLL - 1, UNROLL))
         def _(g):
             for u in range(UNROLL):
-                step(g * UNROLL + u, u % 2)
+                step(begin + g * UNROLL + u, u % 2)
 
     def diagonal(i, n):
         one_i[n] = i
@@ -286,11 +361,12 @@
         one_i[single + e] = 0
         one_j[single + e] = 0
 
-    tiles(first_ref, second_ref, lax.div(targets * (targets - 1), 2), True)
-    tiles(one_i, one_j, single, False)
+    done = firm * (firm - 1) // 2
+    tiles(first_ref, second_ref, done, lax.div(targets * (targets - 1), 2), True)
+    tiles(one_i, one_j, 0, single, False)
 
     def finish(c, _):
-        here = pl.ds(pl.multiple_of(c * TILE, TILE), TILE)
+        here = block_at(c)
         head, tail = acc[0:8, here], acc[8:16, here]
         total = head + pltpu.roll(head, 4, 0) + tail
         res[:, here] = FACTOR * (total - (comp[:, here] - 0.5) * total[3:4])
@@ -298,7 +374,7 @@
 
     lax.fori_loop(0, targets, finish, 0)
 
-    def spread(l, _):
+    def spread(l, side):
         off = offsets[l]
         turn = lax.rem(off, LANES)
         base = pl.multiple_of(off - turn, LANES)
@@ -307,17 +383,23 @@
             res[:, pl.ds(base, LANES)],
             res[:, pl.ds(pl.multiple_of(base + LANES, LANES), LANES)],
         )
-        back = pltpu.roll(both, lax.rem(LANES - turn, LANES), 1)
+        back = pltpu.roll(both, lax.rem(LANES + HALF - turn, LANES), 1)
+        back = jnp.where(lane < HALF, side, back)
         start = pl.multiple_of(l * LANES, LANES)
         accel_ref[:, pl.ds(start, LANES)] = jnp.where(lane < count_ref[l], back, 0.0)[0:3]
         deposit_ref[:, pl.ds(start, LANES)] = jnp.zeros((4, LANES), F32)
+
+    def spread_two(t, _):
+        side = res[:, pl.ds(pl.multiple_of(t * LANES, LANES), LANES)]
+        spread(2 * t, side)
+        spread(2 * t + 1, pltpu.roll(side, HALF, 1))
         return 0
 
-    lax.fori_loop(0, leaves, spread, 0, unroll=8)
+    lax.fori_loop(0, leaves // 2, spread_two, 0, unroll=4)
 
     def valid_slot(s, n):
         slots[n] = s
-        return n + jnp.where(meta_ref[4 * ghosts + s, 1] > 0.5, 1, 0)
+        return n + jnp.where(meta_ref[4 * ghosts + s, 1] > 0, 1, 0)
 
     n_slots = lax.fori_loop(0, owners * SLOTS, valid_slot, jnp.int32(0))
     group = 4
@@ -327,7 +409,7 @@
     def heat(n):
         s = slots[n]
         star = star_ref[s]
-        leaf = meta_ref[4 * ghosts + s, 0].astype(jnp.int32)
+        leaf = meta_ref[4 * ghosts + s, 0]
         there = pl.ds(pl.multiple_of(leaf * LANES, LANES), LANES)
         gas = own_ref[:, there] - 0.5
         h = smooth_ref[pl.ds(leaf, 1), :]
@@ -345,8 +427,8 @@
         )
         p0, p1, p2 = split3(left)
         q0, q1, q2 = split3(right)
-        a = features([p0, p0, p1, p1, p0, p2]).T.astype(BF16)
-        b = features([q0, q1, q0, q1, q2, q0]).astype(BF16)
+        a = stack([p0, p0, p1, p1, p0, p2]).T.astype(BF16)
+        b = stack([q0, q1, q0, q1, q2, q0]).astype(BF16)
         weight = jnp.exp2(nn(a, b))
         share = 1.0 / (1.0 + jnp.sum(weight, axis=0, keepdims=True))
         energy = star[3:4]
@@ -355,7 +437,7 @@
         value = jnp.where(sub < 4, value, 0.0)
         v0, v1, v2 = split3(value)
         v02 = jnp.where(sub < 4, v0, pltpu.roll(v2, 4, 0))
-        v = features([v02, v1]).astype(BF16)
+        v = stack([v02, v1]).astype(BF16)
         hi = weight.astype(BF16)
         lo = (weight - hi.astype(F32)).astype(BF16)
         out = nt(v, hi) + nt(v, lo)
@@ -401,7 +483,7 @@
         gas_position,
         gas_mass.reshape(leaves, LANES),
         leaf_counts,
-        ghost_lists.reshape(-1),
+        ghost_lists[0].T,
         star_position,
         star_energy.reshape(blocks, LANES),
         star_momentum,
@@ -409,23 +491,30 @@
         block_owners.reshape(-1),
         block_leaves,
     )
-    ghost, star, meta = pl.pallas_call(
+    settled = leaves * HALF
+    square = [pltpu.VMEM((TILE, TILE), F32)] * 2 + [pltpu.VMEM((TILE, TILE), BF16)] * 4
+    ghost, star, meta, *early = pl.pallas_call(
         functools.partial(exchange, sizes),
         out_shape=(
             ghost_shape,
             star_shape,
-            jax.ShapeDtypeStruct((4 * ghosts + slots, LANES), F32),
+            jax.ShapeDtypeStruct((4 * ghosts + slots, LANES), jnp.int32),
+            jax.ShapeDtypeStruct((8, settled), F32),
+            jax.ShapeDtypeStruct((settled, FEATURES), BF16),
+            jax.ShapeDtypeStruct((FEATURES, settled), BF16),
+            jax.ShapeDtypeStruct((16, settled), BF16),
+            jax.ShapeDtypeStruct((16, settled), F32),
         ),
-        in_specs=[vmem, vmem],
-        out_specs=(vmem, vmem, vmem),
-        scratch_shapes=[
+        in_specs=[vmem] * 3,
+        out_specs=(vmem,) * 8,
+        scratch_shapes=square + [
             pltpu.SemaphoreType.DMA((4,)),
             pltpu.SemaphoreType.DMA((4,)),
             pltpu.SemaphoreType.DMA((owners,)),
             pltpu.SemaphoreType.DMA((owners,)),
         ],
         compiler_params=pltpu.CompilerParams(collective_id=0, has_side_effects=True),
-    )(ghost_send, star_send)
+    )(own, ghost_send, star_send)
     top = -(-rows // TILE)
     capacity = -(-(rows + 4 * wide) // TILE) * TILE + TILE
     spare = UNROLL + 4
@@ -440,7 +529,7 @@
             jax.ShapeDtypeStruct((3, rows), F32),
             jax.ShapeDtypeStruct((4, rows), F32),
         ),
-        in_specs=[smem, smem, smem, smem, vmem, vmem, vmem, vmem],
+        in_specs=[smem] * 4 + [vmem] * 4 + [pl.BlockSpec(memory_space=pltpu.HBM)] * 5,
         out_specs=(vmem, vmem),
         scratch_shapes=[
             pltpu.VMEM((8, capacity), F32),
@@ -449,20 +538,17 @@
             pltpu.VMEM((16, capacity), BF16),
             pltpu.VMEM((16, capacity + TILE), F32),
             pltpu.VMEM((8, rows + 2 * TILE), F32),
-            pltpu.VMEM((TILE, TILE), F32),
-            pltpu.VMEM((TILE, TILE), F32),
-            pltpu.VMEM((TILE, TILE), BF16),
-            pltpu.VMEM((TILE, TILE), BF16),
-            pltpu.VMEM((TILE, TILE), BF16),
-            pltpu.VMEM((TILE, TILE), BF16),
+            *square,
             pltpu.SMEM((leaves,), jnp.int32),
             pltpu.SMEM((singles,), jnp.int32),
             pltpu.SMEM((singles,), jnp.int32),
             pltpu.SMEM((slots + 4,), jnp.int32),
+            pltpu.SemaphoreType.DMA((5,)),
         ],
     )(
         leaf_counts, meta, first, second,
         own, gas_smoothing.reshape(leaves, LANES), ghost, star.reshape(slots, 8, LANES),
+        *early,
     )
 
 

time: 42.7 us -> 38.9 us (0.911)
  Pallas kernels: 40.5 us -> 37.8 us
  local copies, waits for them, and re-layouts: 1.36 us -> 0 us
    pallas_call x1, Pallas kernels: 27.2 us -> 23.1 us  [on_device(): pl.pallas_call(functools.partial(gravity, sizes), out_shape=(jax.ShapeDty...]
    pallas_call x1, Pallas kernels: 11.2 us -> 12.7 us  [on_device(): pl.pallas_call(functools.partial(exchange, sizes), out_shape=(ghost_shape...]
    unnamed x3 -> x0, local copies, waits for them, and re-layouts: 0.76 us -> none
    reshape x1 -> x0, local copies, waits for them, and re-layouts: 0.6 us -> none  [on_device(): ghost_lists.reshape(-1)]
where the time goes in v2:
time: 38.9 us; the launch traced here: 38.5 us
  Pallas kernels  37.8 us (97%)
  between operations  0.64 us (2%)
    pallas_call x1, Pallas kernels, on_device(): pl.pallas_call(functools.partial(gravity, sizes), out_shape=(jax.ShapeDty...  23.1 us
    pallas_call x1, Pallas kernels, on_device(): pl.pallas_call(functools.partial(exchange, sizes), out_shape=(ghost_shape...  12.7 us
    pallas_call x1, Pallas kernels, on_device(): pl.pallas_call(functools.partial(prepare_sends, sizes), out_shape=(jax.Sh...  2.03 us

profile of v2, /device:TPU:0, one launch (start us, length us, event | category | flops | bytes accessed | tf_op | source)
XLA Modules:
  0.0 38.5 jit_solution(7263245409750958083)
XLA Ops:
  0.6 2.0 %shard_map.140 = (f32[8,4096]{1,0:T(8,128)}, f32[4,8,256]{2,1,0:T(8,128)}, f32[8,3,8,128]{3,2,1,0:T(8,128)}) custom-call(f32[3,4096]{1,0:T(4,128)} %pos_ref.1, f32[32,128]{1,0:T(8,128)} %bitcast.10, s32[32]{0:T(128)} %count_ref.3, s32[2,4]{1,0:T(2,128)} %bitcast.12, f32[3,2048]{1,0:T(4,128)} %star_pos_ref.1, f32[16,128]{1,0:T(8,128)} %bitcast.11, ...), custom_call_target="tpu_custom_call" | custom-call | tf_op jit(solution)/shard_map/pallas_call | solution.py:477
  2.7 12.7 %shard_map.141 = (f32[4,8,256]{2,1,0:T(8,128)}, f32[8,3,8,128]{3,2,1,0:T(8,128)}, s32[32,128]{1,0:T(8,128)}, f32[8,2048]{1,0:T(8,128)}, bf16[2048,48]{1,0:T(8,12...) custom-call(f32[8,4096]{1,0:T(8,128)} %get-tuple-element.13.own.own_ref, ...), custom_call_target="tpu_custom_call" | custom-call | tf_op jit(solution)/shard_map/pallas_call | solution.py:496
  15.4 23.1 %shard_map.142 = (f32[3,4096]{1,0:T(4,128)}, f32[4,4096]{1,0:T(4,128)}) custom-call(s32[32]{0:T(128)} %count_ref.3, s32[32,128]{1,0:T(8,128)} %get-tuple-element.16.meta_ref, s32[148]{0:T(256)} %constant.4.clone.first_ref, s32[148]{0:T(256)} %constant.5.clone.second_ref, f32[8,4096]{1,0:T(8,128)} %get-tuple-element.13.own.own_ref, f32[32,128]{1,0:T(8,128)} %bitcast.9, ...), custom_call_target="tpu_custom_call" | custom-call | tf_op jit(solution)/shard_map/pallas_call | solution.py:526

commit v3 on v2

--- a/solution.py
+++ b/solution.py
@@ -27,6 +27,7 @@
 TILE = 256
 FEATURES = 48
 UNROLL = 8
+GROUP = 8
 
 
 def split3(x):
@@ -214,26 +215,33 @@
 
     distance, high, low = (d0, d1), (h0, h1), (l0, l1)
 
-    def pair(p):
+    period = firm + 1
+    unroll = 2 * period
+    assert firm % 4 == 0
+
+    def task(g, e):
+        g, e = g + e // unroll, e % unroll
+        half, r = divmod(e, period)
+        middle = (firm - 1) // 2
+        if r in (middle, firm):
+            i = (4 * g + 2 * half + r // firm) % firm
+            return i, i, False
+        p = (2 * g + half) * (firm - 1) + r - r // (middle + 1)
         i = p % firm
-        return i, (i + 1 + p // firm) % firm
-
-    count = firm * (firm - 1) // 2
-    distances(*pair(0), d0, side_a, side_b)
+        return i, (i + 1 + p // firm) % firm, True
+
+    distances(*task(0, 0)[:2], d0, side_a, side_b)
+    distances(*task(0, 1)[:2], d1, side_a, side_b)
     kernel_values(d0, h0, l0)
-    distances(*pair(1), d1, side_a, side_b)
-    unroll = next(u for u in (14, 10, 8, 6, 4, 2, 1) if count % u == 0)
-    assert unroll % 2 == 0
-
-    @pl.loop(0, count // unroll)
+
+    @pl.loop(0, firm // 4)
     def _(g):
         for e in range(unroll):
-            p = g * unroll + e
-            i, j = pair(p)
             even = e % 2
-            accumulate(i, j, i, j, high[even], low[even], weights, acc, True)
+            i, j, both = task(g, e)
+            distances(*task(g, e + 2)[:2], distance[even], side_a, side_b)
             kernel_values(distance[1 - even], high[1 - even], low[1 - even])
-            distances(*pair(p + 2), distance[even], side_a, side_b)
+            accumulate(i, j, i, j, high[even], low[even], weights, acc, both)
 
     for k in range(4):
         ghost_copy(k).wait()
@@ -261,6 +269,7 @@
     accel_ref, deposit_ref,
     comp, side_a, side_b, weights, acc, res,
     d0, d1, h0, h1, l0, l1,
+    star_a, star_b, star_d, star_h, star_l, star_v,
     offsets, one_i, one_j, slots, sems,
 ):
     n_x, n_y, n_z, leaves, ghosts, blocks = sizes
@@ -327,43 +336,64 @@
 
     distance, high, low = (d0, d1), (h0, h1), (l0, l1)
 
-    def tiles(table_i, table_j, begin, count, both):
-        def step(p, even):
-            q = jnp.maximum(p - 2, begin)
-            valid = jnp.logical_and(p >= begin + 2, p - 2 < count)
+    def tiles(tables, unroll):
+        kinds = len(tables)
+        steps = 0
+        for table_i, table_j, begin, count, both in tables:
+            steps = jnp.maximum(steps, kinds * (count - begin) + 2)
+
+        def entry(u, base, ahead):
+            table_i, table_j, begin, count, both = tables[(u + ahead) % kinds]
+            k = begin + base + (u + ahead) // kinds
+            return table_i, table_j, begin, count, both, k
+
+        def step(base, u):
+            even = u % 2
+            table_i, table_j, *_, k = entry(u, base, 0)
+            distances(table_i[k], table_j[k], distance[even], side_a, side_b)
+            kernel_values(distance[1 - even], high[1 - even], low[1 - even])
+            table_i, table_j, begin, count, both, k = entry(u, base, -2)
+            valid = jnp.logical_and(k >= begin, k < count)
+            q = jnp.maximum(k, begin)
             i, j = table_i[q], table_j[q]
             to_i, to_j = jnp.where(valid, i, trash), jnp.where(valid, j, trash)
             accumulate(i, j, to_i, to_j, high[even], low[even], weights, acc, both)
-            kernel_values(distance[1 - even], high[1 - even], low[1 - even])
-            distances(table_i[p], table_j[p], distance[even], side_a, side_b)
-
-        @pl.loop(0, lax.div(count - begin + 2 + UNROLL - 1, UNROLL))
+
+        @pl.loop(0, lax.div(steps + (unroll - 1), unroll))
         def _(g):
-            for u in range(UNROLL):
-                step(begin + g * UNROLL + u, u % 2)
-
-    def diagonal(i, n):
+            for u in range(unroll):
+                step(g * (unroll // kinds), u)
+
+    def single(i, j, n):
         one_i[n] = i
-        one_j[n] = i
+        one_j[n] = j
         return n + 1
 
     def column(s, n):
-        def entry(i, n):
-            one_i[n] = i
-            one_j[n] = s
-            return n + 1
-
-        return lax.fori_loop(0, targets, entry, n)
-
-    single = lax.fori_loop(0, targets, diagonal, jnp.int32(0))
-    single = lax.fori_loop(targets, sources, column, single)
-    for e in range(UNROLL + 2):
-        one_i[single + e] = 0
-        one_j[single + e] = 0
+        return lax.fori_loop(0, targets, lambda i, n: single(i, s, n), n)
 
     done = firm * (firm - 1) // 2
-    tiles(first_ref, second_ref, done, lax.div(targets * (targets - 1), 2), True)
-    tiles(one_i, one_j, 0, single, False)
+    n_both = lax.div(targets * (targets - 1), 2) - done
+    n_one = lax.fori_loop(firm, targets, lambda i, n: single(i, i, n), jnp.int32(0))
+    n_one = lax.fori_loop(targets, sources, column, n_one)
+
+    def blank(n, _):
+        one_i[n] = 0
+        one_j[n] = 0
+        return 0
+
+    lax.fori_loop(n_one, jnp.maximum(n_one, n_both) + UNROLL + 2, blank, 0)
+    tiles(
+        [
+            (first_ref, second_ref, done, done + n_both, True),
+            (one_i, one_j, 0, jnp.minimum(n_one, n_both), False),
+        ],
+        UNROLL,
+    )
+
+    @pl.when(n_one > n_both)
+    def _():
+        tiles([(one_i, one_j, n_both, n_one, False)], UNROLL // 2)
 
     def finish(c, _):
         here = block_at(c)
@@ -402,16 +432,20 @@
         return n + jnp.where(meta_ref[4 * ghosts + s, 1] > 0, 1, 0)
 
     n_slots = lax.fori_loop(0, owners * SLOTS, valid_slot, jnp.int32(0))
-    group = 4
-    for e in range(group):
-        slots[n_slots + e] = 0
-
-    def heat(n):
+    def empty_slot(e, _):
+        slots[e] = 0
+        return 0
+
+    lax.fori_loop(n_slots, n_slots + GROUP + 3, empty_slot, 0)
+
+    def slot_at(n):
         s = slots[n]
-        star = star_ref[s]
         leaf = meta_ref[4 * ghosts + s, 0]
         there = pl.ds(pl.multiple_of(leaf * LANES, LANES), LANES)
-        gas = own_ref[:, there] - 0.5
+        return star_ref[s], own_ref[:, there] - 0.5, leaf, there
+
+    def star_features(n, left_out, right_out):
+        star, gas, leaf, _ = slot_at(n)
         h = smooth_ref[pl.ds(leaf, 1), :]
         inverse = LOG2E / (h * h)
         ys = star - 0.5
@@ -427,33 +461,47 @@
         )
         p0, p1, p2 = split3(left)
         q0, q1, q2 = split3(right)
-        a = stack([p0, p0, p1, p1, p0, p2]).T.astype(BF16)
-        b = stack([q0, q1, q0, q1, q2, q0]).astype(BF16)
-        weight = jnp.exp2(nn(a, b))
+        left_out[...] = stack([p0, p0, p1, p1, p0, p2]).T.astype(BF16)
+        right_out[...] = stack([q0, q1, q0, q1, q2, q0]).astype(BF16)
+
+    def star_weights(n, exponent, high, low, value_out):
+        weight = jnp.exp2(exponent[...])
+        hi = weight.astype(BF16)
+        high[...] = hi
+        low[...] = (weight - hi.astype(F32)).astype(BF16)
         share = 1.0 / (1.0 + jnp.sum(weight, axis=0, keepdims=True))
+        star = star_ref[slots[n]]
         energy = star[3:4]
         momentum = pltpu.roll(star, 4, 0)
-        value = jnp.where(sub < 3, momentum - RADIAL_PUSH * energy * ys, energy) * share
-        value = jnp.where(sub < 4, value, 0.0)
-        v0, v1, v2 = split3(value)
+        value = jnp.where(sub < 3, momentum - RADIAL_PUSH * energy * (star - 0.5), energy)
+        v0, v1, v2 = split3(jnp.where(sub < 4, value * share, 0.0))
         v02 = jnp.where(sub < 4, v0, pltpu.roll(v2, 4, 0))
-        v = stack([v02, v1]).astype(BF16)
-        hi = weight.astype(BF16)
-        lo = (weight - hi.astype(F32)).astype(BF16)
-        out = nt(v, hi) + nt(v, lo)
+        value_out[...] = stack([v02, v1]).astype(BF16)
+
+    def star_deposit(n, high, low, value):
+        _, gas, leaf, there = slot_at(jnp.maximum(n, 0))
+        v = value[...]
+        out = nt(v, high[...]) + nt(v, low[...])
         head, tail = out[0:8], out[8:16]
         total = head + pltpu.roll(head, 4, 0) + tail
         heat_here = total[3:4]
         kick = pltpu.roll(total + RADIAL_PUSH * heat_here * gas, 1, 0)
         both = jnp.where(sub == 0, heat_here, kick)
-        live = jnp.where(n < n_slots, count_ref[leaf], 0)
-        return there, jnp.where(lane < live, both, 0.0)[0:4]
-
-    @pl.loop(0, lax.div(n_slots + group - 1, group))
+        valid = jnp.logical_and(n >= 0, n < n_slots)
+        live = jnp.where(valid, count_ref[leaf], 0)
+        deposit_ref[:, there] = deposit_ref[:, there] + jnp.where(lane < live, both, 0.0)[0:4]
+
+    @pl.loop(0, lax.div(n_slots + 3 + GROUP - 1, GROUP))
     def _(t):
-        done = [heat(t * group + e) for e in range(group)]
-        for there, add in done:
-            deposit_ref[:, there] = deposit_ref[:, there] + add
+        for e in range(GROUP):
+            n, even = t * GROUP + e, e % 2
+            star_features(n, star_a.at[even], star_b.at[even])
+            star_d[even] = nn(star_a[1 - even], star_b[1 - even])
+            star_weights(
+                jnp.maximum(n - 2, 0), star_d.at[1 - even],
+                star_h.at[1 - even], star_l.at[1 - even], star_v.at[1 - even],
+            )
+            star_deposit(n - 3, star_h.at[even], star_l.at[even], star_v.at[even])
 
 
 def on_device(
@@ -522,7 +570,7 @@
     pairs = pairs + [(0, 0)] * spare
     first = jnp.asarray(np.array([a for a, _ in pairs], np.int32))
     second = jnp.asarray(np.array([b for _, b in pairs], np.int32))
-    singles = (capacity // TILE) * top + spare
+    singles = (capacity // TILE) * top + spare + UNROLL
     return pl.pallas_call(
         functools.partial(gravity, sizes),
         out_shape=(
@@ -539,10 +587,16 @@
             pltpu.VMEM((16, capacity + TILE), F32),
             pltpu.VMEM((8, rows + 2 * TILE), F32),
             *square,
+            pltpu.VMEM((2, LANES, FEATURES), BF16),
+            pltpu.VMEM((2, FEATURES, LANES), BF16),
+            pltpu.VMEM((2, LANES, LANES), F32),
+            pltpu.VMEM((2, LANES, LANES), BF16),
+            pltpu.VMEM((2, LANES, LANES), BF16),
+            pltpu.VMEM((2, 16, LANES), BF16),
             pltpu.SMEM((leaves,), jnp.int32),
             pltpu.SMEM((singles,), jnp.int32),
             pltpu.SMEM((singles,), jnp.int32),
-            pltpu.SMEM((slots + 4,), jnp.int32),
+            pltpu.SMEM((slots + GROUP + 3,), jnp.int32),
             pltpu.SemaphoreType.DMA((5,)),
         ],
     )(

time: 38.9 us -> 32.8 us (0.84)
  Pallas kernels: 37.8 us -> 31.9 us
    pallas_call x1, Pallas kernels: 23.1 us -> 17.1 us  [on_device(): pl.pallas_call(functools.partial(gravity, sizes), out_shape=(jax.ShapeDty...]
where the time goes in v3:
time: 32.8 us; the launch traced here: 32.6 us
  Pallas kernels  31.9 us (97%)
  between operations  0.64 us (2%)
    pallas_call x1, Pallas kernels, on_device(): pl.pallas_call(functools.partial(gravity, sizes), out_shape=(jax.ShapeDty...  17.1 us
    pallas_call x1, Pallas kernels, on_device(): pl.pallas_call(functools.partial(exchange, sizes), out_shape=(ghost_shape...  12.9 us
    pallas_call x1, Pallas kernels, on_device(): pl.pallas_call(functools.partial(prepare_sends, sizes), out_shape=(jax.Sh...  2.03 us

profile of v3, /device:TPU:0, one launch (start us, length us, event | category | flops | bytes accessed | tf_op | source)
XLA Modules:
  0.0 32.6 jit_solution(1201923228601034212)
XLA Ops:
  0.6 2.0 %shard_map.140 = (f32[8,4096]{1,0:T(8,128)}, f32[4,8,256]{2,1,0:T(8,128)}, f32[8,3,8,128]{3,2,1,0:T(8,128)}) custom-call(f32[3,4096]{1,0:T(4,128)} %pos_ref.1, f32[32,128]{1,0:T(8,128)} %bitcast.10, s32[32]{0:T(128)} %count_ref.3, s32[2,4]{1,0:T(2,128)} %bitcast.12, f32[3,2048]{1,0:T(4,128)} %star_pos_ref.1, f32[16,128]{1,0:T(8,128)} %bitcast.11, ...), custom_call_target="tpu_custom_call" | custom-call | tf_op jit(solution)/shard_map/pallas_call | solution.py:525
  2.7 12.9 %shard_map.141 = (f32[4,8,256]{2,1,0:T(8,128)}, f32[8,3,8,128]{3,2,1,0:T(8,128)}, s32[32,128]{1,0:T(8,128)}, f32[8,2048]{1,0:T(8,128)}, bf16[2048,48]{1,0:T(8,12...) custom-call(f32[8,4096]{1,0:T(8,128)} %get-tuple-element.13.own.own_ref, ...), custom_call_target="tpu_custom_call" | custom-call | tf_op jit(solution)/shard_map/pallas_call | solution.py:544
  15.5 17.1 %shard_map.142 = (f32[3,4096]{1,0:T(4,128)}, f32[4,4096]{1,0:T(4,128)}) custom-call(s32[32]{0:T(128)} %count_ref.3, s32[32,128]{1,0:T(8,128)} %get-tuple-element.16.meta_ref, s32[148]{0:T(256)} %constant.4.clone.first_ref, s32[148]{0:T(256)} %constant.5.clone.second_ref, f32[8,4096]{1,0:T(8,128)} %get-tuple-element.13.own.own_ref, f32[32,128]{1,0:T(8,128)} %bitcast.9, ...), custom_call_target="tpu_custom_call" | custom-call | tf_op jit(solution)/shard_map/pallas_call | solution.py:574
